TPU v7x, 32 devices: a whole 2x2x4 slice. The times are simulated.
32 devices in a mesh: ctx: 8 (over y, x, core), dp: 4 (over z).
Axes of the slice: x: 2, y: 2, z: 4, core: 2. Of those that a mesh axis runs over, the one named last changes fastest.
Arguments:
- query: bfloat16 [4, 1024, 512], P('dp', 'ctx'), may hold values from -6 to 6
- key_input: bfloat16 [4, 1024, 512], P('dp', 'ctx'), may hold values from -6 to 6
- value_input: bfloat16 [4, 1024, 512], P('dp', 'ctx'), may hold values from -6 to 6
- filter_taps: float32 [1024, 512], P('ctx'), may hold values from -6 to 6
- grad_output: bfloat16 [4, 1024, 512], P('dp', 'ctx'), may hold values from -6 to 6
Outputs:
- output: bfloat16 [4, 1024, 512], P('dp', 'ctx')
- grad_query: bfloat16 [4, 1024, 512], P('dp', 'ctx')
- grad_key: bfloat16 [4, 1024, 512], P('dp', 'ctx')
- grad_value: bfloat16 [4, 1024, 512], P('dp', 'ctx')
- grad_filter: float32 [1024, 512], P('ctx')
All inputs are finite; a program needn't handle non-finite values.
Results may differ from a plain program's by a relative error of at most 0.0058.
Values may be sent and summed in bfloat16 or wider, within the bound.
A program may use at most 64 MiB of HBM per device.

v0:
```python
import functools
import math

import jax
import jax.numpy as jnp
import numpy as np
from jax import lax
from jax.experimental import pallas as pl
from jax.experimental.pallas import tpu as pltpu
from jax.sharding import PartitionSpec as P

HIGH = lax.Precision.HIGHEST
MESH = pl.DeviceIdType.MESH
LANES = 128
F32 = jnp.float32
BF16 = jnp.bfloat16


def block_tables(length):
    odd = 2 * np.arange(length, dtype=np.int64)[:, None] + 1
    angle = (odd * np.arange(length, dtype=np.int64)[None, :] % (4 * length)) * (2.0 * math.pi / (4 * length))
    ahead = np.concatenate([np.cos(angle), -np.sin(angle)], axis=0).astype(np.float32)
    back = ahead.T / np.float32(length)

    def split(table):
        high = jnp.asarray(table).astype(BF16)
        low = (jnp.asarray(table) - high.astype(F32)).astype(BF16)
        return high, low

    with jax.ensure_compile_time_eval():
        ahead_high, ahead_low = split(ahead)
        back_high, back_low = split(back)
        return (
            np.asarray(jnp.concatenate([ahead_high, ahead_low], axis=1)),
            np.asarray(jnp.concatenate([back_high, back_low], axis=1)),
        )


def merge(first, second, low):
    half = first.shape[-1] // 2
    turned = pltpu.roll(jnp.where(low, second, first), half, 1)
    return jnp.where(low, first, turned), jnp.where(low, turned, second)


def kernel(
    nctx,
    ndp,
    q_ref,
    k_ref,
    v_ref,
    f_ref,
    g_ref,
    ahead_ref,
    back_ref,
    out_ref,
    gq_ref,
    gk_ref,
    gv_ref,
    gf_ref,
    send1,
    rx1,
    sig,
    wei,
    oth,
    gfs,
    rs_send,
    rs_rx,
    g2_send,
    g2_rx,
    mg_send,
    mg_rx,
    s1_send,
    s1_recv,
    rs_ssem,
    rs_rsem,
    g2_ssem,
    g2_rsem,
    mg_ssem,
    mg_rsem,
):
    me = lax.axis_index("ctx")
    row = lax.axis_index("dp")
    length = q_ref.shape[1]
    hl = length // 2
    tiles = nctx // 2

    barrier = pltpu.get_barrier_semaphore()
    for oc in range(nctx):
        for od in range(ndp):
            if oc or od:
                pl.semaphore_signal(
                    barrier,
                    inc=1,
                    device_id={"ctx": lax.rem(me + oc, nctx), "dp": lax.rem(row + od, ndp)},
                    device_id_type=MESH,
                )

    low = lax.broadcasted_iota(jnp.int32, (length, LANES), 1) < LANES // 2
    low_h = lax.broadcasted_iota(jnp.int32, (hl, LANES), 1) < LANES // 2
    for p in range(tiles):
        cols = slice(p * LANES, (p + 1) * LANES)
        x = (k_ref[0, :, cols].astype(F32) * v_ref[0, :, cols].astype(F32)).astype(BF16).astype(F32)
        g = (g_ref[0, :, cols].astype(F32) * q_ref[0, :, cols].astype(F32)).astype(BF16).astype(F32)
        even, odd = merge(x, g, low)
        send1[2 * p, 0:length, :] = even.astype(BF16)
        send1[2 * p + 1, 0:length, :] = odd.astype(BF16)
        even, odd = merge(f_ref[0:hl, cols], f_ref[hl:length, cols], low_h)
        send1[2 * p, length : length + hl, :] = even.astype(BF16)
        send1[2 * p + 1, length : length + hl, :] = odd.astype(BF16)

    pl.semaphore_wait(barrier, nctx * ndp - 1)

    def copy1(peer, slot):
        return pltpu.make_async_remote_copy(
            src_ref=send1.at[peer],
            dst_ref=rx1.at[slot],
            send_sem=s1_send.at[peer],
            recv_sem=s1_recv.at[slot],
            device_id={"ctx": peer, "dp": row},
            device_id_type=MESH,
        )

    order = [nctx // 2 + o for o in range(nctx // 2)] + list(range(1, nctx // 2))
    peers = [lax.rem(me + o, nctx) for o in order]
    for peer in peers:
        copy1(peer, me).start()
    rx1[pl.ds(me, 1)] = send1[pl.ds(me, 1)]

    def transform(src):
        z = rx1[src, 0:length, :]
        fa = rx1[src, length : length + hl, :].astype(F32)
        turned = pltpu.roll(fa, LANES // 2, 1)
        w = jnp.concatenate([jnp.where(low_h, fa, turned), jnp.where(low_h, turned, fa)], axis=0).astype(BF16)
        both = jnp.concatenate([z, w], axis=1)
        spec = jnp.dot(ahead_ref[...], jnp.concatenate([both, both], axis=0), preferred_element_type=F32)
        sig[src] = spec[:, 0:LANES]
        wei[src] = spec[:, LANES:]

    transform(me)
    for peer in reversed(peers):
        copy1(peer, peer).wait_recv()
        transform(peer)

    lane8 = lax.broadcasted_iota(jnp.int32, (8, LANES), 1) < LANES // 2
    parity = lax.rem(lax.broadcasted_iota(jnp.int32, (8, LANES), 0), 2)
    alt = jnp.where(parity == 0, 1.0, -1.0).astype(F32)
    lane_sign = jnp.where(lane8, 1.0, -1.0).astype(F32)
    both_sign = alt * lane_sign

    @pl.loop(0, length // 8)
    def _(i):
        re = pl.ds(pl.multiple_of(i * 8, 8), 8)
        im = pl.ds(pl.multiple_of(length + i * 8, 8), 8)
        s_re = [sig[d, re, :] for d in range(nctx)]
        s_im = [sig[d, im, :] for d in range(nctx)]
        u_re = [jnp.where(lane8, pltpu.roll(a, LANES // 2, 1), a) for a in s_re]
        u_im = [jnp.where(lane8, pltpu.roll(a, LANES // 2, 1), a) for a in s_im]
        x_re = [s_re[0]] + [s_re[n] - alt * s_im[n - 1] for n in range(1, nctx)]
        x_im = [s_im[0]] + [s_im[n] + alt * s_re[n - 1] for n in range(1, nctx)]
        v_re = [jnp.where(lane8, x_re[n], 0.0) for n in range(tiles)]
        v_im = [jnp.where(lane8, x_im[n], 0.0) for n in range(tiles)]
        for n in range(tiles, nctx):
            v_re.append(jnp.where(lane8, x_re[n], pltpu.roll(x_re[n - tiles], LANES // 2, 1)))
            v_im.append(jnp.where(lane8, x_im[n], pltpu.roll(x_im[n - tiles], LANES // 2, 1)))
        for j in range(tiles):
            a_re = jnp.zeros((8, LANES), F32)
            a_im = jnp.zeros((8, LANES), F32)
            for m in range(j, nctx):
                n = m - j
                a_re = a_re + u_re[m] * v_re[n] + u_im[m] * v_im[n]
                a_im = a_im + u_im[m] * v_re[n] - u_re[m] * v_im[n]
            gfs[j, re, :] = a_re
            gfs[j, im, :] = a_im

    def inverse(spec):
        high = spec.astype(BF16)
        return jnp.dot(back_ref[...], jnp.concatenate([high, high], axis=0), preferred_element_type=F32)

    def copy_rs(peer, slot):
        return pltpu.make_async_remote_copy(
            src_ref=rs_send.at[peer],
            dst_ref=rs_rx.at[slot],
            send_sem=rs_ssem.at[peer],
            recv_sem=rs_rsem.at[slot],
            device_id={"ctx": me, "dp": peer},
            device_id_type=MESH,
        )

    for j in range(tiles):
        rs_send[j] = inverse(gfs[j]).astype(BF16)
    rows_peers = [lax.rem(row + o, ndp) for o in range(1, ndp)]
    for peer in rows_peers:
        copy_rs(peer, row).start()

    @pl.loop(0, length // 8)
    def _(i):
        re = pl.ds(pl.multiple_of(i * 8, 8), 8)
        im = pl.ds(pl.multiple_of(length + i * 8, 8), 8)
        s_re = [sig[d, re, :] for d in range(nctx)]
        s_im = [sig[d, im, :] for d in range(nctx)]
        q_re = [jnp.where(lane8, s_re[n], s_re[nctx - 1 - n]) for n in range(nctx)]
        q_im = [jnp.where(lane8, s_im[n], s_im[nctx - 1 - n]) for n in range(nctx)]
        z_re = [q_re[0]] + [q_re[n] - both_sign * q_im[n - 1] for n in range(1, nctx)]
        z_im = [q_im[0]] + [q_im[n] + both_sign * q_re[n - 1] for n in range(1, nctx)]
        w_re = [wei[d, re, :] for d in range(nctx)]
        w_im = [wei[d, im, :] * lane_sign for d in range(nctx)]
        o_re, o_im = [], []
        for n in range(nctx):
            a_re = jnp.zeros((8, LANES), F32)
            a_im = jnp.zeros((8, LANES), F32)
            for j in range(n + 1):
                a_re = a_re + w_re[j] * z_re[n - j] - w_im[j] * z_im[n - j]
                a_im = a_im + w_re[j] * z_im[n - j] + w_im[j] * z_re[n - j]
            o_re.append(a_re)
            o_im.append(a_im)
        for d in range(nctx):
            oth[d, re, :] = jnp.where(lane8, o_re[d], o_re[nctx - 1 - d])
            oth[d, im, :] = jnp.where(lane8, o_im[d], o_im[nctx - 1 - d])

    def copy_mg(peer, slot):
        return pltpu.make_async_remote_copy(
            src_ref=mg_send.at[peer],
            dst_ref=mg_rx.at[slot],
            send_sem=mg_ssem.at[peer],
            recv_sem=mg_rsem.at[slot],
            device_id={"ctx": peer, "dp": row},
            device_id_type=MESH,
        )

    for at, peer in enumerate(peers):
        mg_send[peer] = inverse(oth[peer]).astype(BF16)
        if at:
            copy_mg(peers[at - 1], me).start()
    mg_rx[me] = inverse(oth[me]).astype(BF16)
    copy_mg(peers[-1], me).start()

    total = rs_send[row].astype(F32)
    for peer in rows_peers:
        copy_rs(peer, peer).wait_recv()
        total = total + rs_rx[peer].astype(F32)
    first, second = merge(total[0:hl], total[hl:length], low_h)
    g2_send[0] = first.astype(BF16)
    g2_send[1] = second.astype(BF16)

    def copy_g2(part, to_row, slot):
        return pltpu.make_async_remote_copy(
            src_ref=g2_send.at[part],
            dst_ref=g2_rx.at[slot],
            send_sem=g2_ssem.at[part, to_row],
            recv_sem=g2_rsem.at[slot],
            device_id={"ctx": row + part * tiles, "dp": to_row},
            device_id_type=MESH,
        )

    for part in range(2):
        for o in range(1, ndp):
            copy_g2(part, lax.rem(row + o, ndp), me).start()
        mine = me == row + part * tiles

        @pl.when(mine)
        def _():
            g2_rx[me] = g2_send[part]

        @pl.when(jnp.logical_not(mine))
        def _():
            copy_g2(part, row, me).start()

    for peer in peers:
        copy_mg(peer, peer).wait_recv()
    for p in range(tiles):
        cols = slice(p * LANES, (p + 1) * LANES)
        mixed, back = merge(mg_rx[2 * p].astype(F32), mg_rx[2 * p + 1].astype(F32), low)
        out_ref[0, :, cols] = (q_ref[0, :, cols].astype(F32) * mixed).astype(BF16)
        gq_ref[0, :, cols] = (g_ref[0, :, cols].astype(F32) * mixed).astype(BF16)
        gk_ref[0, :, cols] = (v_ref[0, :, cols].astype(F32) * back).astype(BF16)
        gv_ref[0, :, cols] = (k_ref[0, :, cols].astype(F32) * back).astype(BF16)

    from_row = lax.rem(me, tiles)
    for c in range(nctx):
        outside = jnp.logical_not(jnp.logical_and(me == c, row == from_row))

        @pl.when(outside)
        def _():
            copy_g2(0, row, c).wait_recv()

    for p in range(tiles):
        cols = slice(p * LANES, (p + 1) * LANES)
        top, bottom = merge(g2_rx[2 * p].astype(F32), g2_rx[2 * p + 1].astype(F32), low_h)
        gf_ref[0:hl, cols] = top
        gf_ref[hl:length, cols] = bottom

    for peer in peers:
        copy1(peer, me).wait_send()
        copy_mg(peer, me).wait_send()
    for peer in rows_peers:
        copy_rs(peer, row).wait_send()
    for part in range(2):
        for o in range(1, ndp):
            copy_g2(part, lax.rem(row + o, ndp), me).wait_send()

        @pl.when(jnp.logical_not(me == row + part * tiles))
        def _():
            copy_g2(part, row, me).wait_send()


def fused(nctx, ndp, query, key_input, value_input, filter_taps, grad_output):
    length, channels = query.shape[1], query.shape[2]
    ahead, back = block_tables(length)
    vm = pl.BlockSpec(memory_space=pltpu.VMEM)
    wide = jax.ShapeDtypeStruct(query.shape, BF16)
    hl, tiles = length // 2, nctx // 2
    dma = pltpu.SemaphoreType.DMA
    return pl.pallas_call(
        functools.partial(kernel, nctx, ndp),
        out_shape=(wide, wide, wide, wide, jax.ShapeDtypeStruct((length, channels), F32)),
        in_specs=[vm] * 7,
        out_specs=(vm,) * 5,
        scratch_shapes=[
            pltpu.VMEM((nctx, length + hl, LANES), BF16),
            pltpu.VMEM((nctx, length + hl, LANES), BF16),
            pltpu.VMEM((nctx, 2 * length, LANES), F32),
            pltpu.VMEM((nctx, 2 * length, LANES), F32),
            pltpu.VMEM((nctx, 2 * length, LANES), F32),
            pltpu.VMEM((tiles, 2 * length, LANES), F32),
            pltpu.VMEM((tiles, length, LANES), BF16),
            pltpu.VMEM((ndp, length, LANES), BF16),
            pltpu.VMEM((2, hl, LANES), BF16),
            pltpu.VMEM((nctx, hl, LANES), BF16),
            pltpu.VMEM((nctx, length, LANES), BF16),
            pltpu.VMEM((nctx, length, LANES), BF16),
            dma((nctx,)),
            dma((nctx,)),
            dma((ndp,)),
            dma((ndp,)),
            dma((2, ndp)),
            dma((nctx,)),
            dma((nctx,)),
            dma((nctx,)),
        ],
        compiler_params=pltpu.CompilerParams(collective_id=0, has_side_effects=True),
    )(query, key_input, value_input, filter_taps, grad_output, jnp.asarray(ahead), jnp.asarray(back))


def build_tables(length):
    padded = 2 * length
    columns = 1
    while columns * columns < padded and length % (2 * columns) == 0:
        columns = columns * 2
    row_count = padded // columns
    col_index = jnp.arange(columns, dtype=jnp.int32)
    row_index = jnp.arange(row_count, dtype=jnp.int32)
    col_angle = (col_index[:, None] * col_index[None, :] % columns).astype(jnp.float32) * (
        2.0 * math.pi / columns
    )
    row_angle = (row_index[:, None] * row_index[None, :] % row_count).astype(jnp.float32) * (
        2.0 * math.pi / row_count
    )
    twist_angle = (row_index[:, None] * col_index[None, :] % padded).astype(jnp.float32) * (
        2.0 * math.pi / padded
    )
    return (
        jnp.cos(col_angle),
        -jnp.sin(col_angle),
        jnp.cos(row_angle),
        -jnp.sin(row_angle),
        jnp.cos(twist_angle),
        -jnp.sin(twist_angle),
        row_count,
        columns,
        padded,
    )


def forward(signal, tables):
    col_real, col_imag, row_real, row_imag, twist_real, twist_imag, row_count, columns, padded = (
        tables
    )
    half_rows = row_count // 2
    blocks = signal.reshape(signal.shape[0], half_rows, columns, signal.shape[2])
    section_real = jnp.einsum("kn,snac->scka", row_real[:, :half_rows], blocks, precision=HIGH)
    section_imag = jnp.einsum("kn,snac->scka", row_imag[:, :half_rows], blocks, precision=HIGH)
    turned_real = section_real * twist_real - section_imag * twist_imag
    turned_imag = section_real * twist_imag + section_imag * twist_real
    spec_real = jnp.einsum("scka,aj->sckj", turned_real, col_real, precision=HIGH) - jnp.einsum(
        "scka,aj->sckj", turned_imag, col_imag, precision=HIGH
    )
    spec_imag = jnp.einsum("scka,aj->sckj", turned_real, col_imag, precision=HIGH) + jnp.einsum(
        "scka,aj->sckj", turned_imag, col_real, precision=HIGH
    )
    return (spec_real, spec_imag)


def inverse(spec, tables):
    col_real, col_imag, row_real, row_imag, twist_real, twist_imag, row_count, columns, padded = (
        tables
    )
    spec_real, spec_imag = spec
    half_rows = row_count // 2
    section_real = jnp.einsum("scka,aj->sckj", spec_real, col_real, precision=HIGH) + jnp.einsum(
        "scka,aj->sckj", spec_imag, col_imag, precision=HIGH
    )
    section_imag = jnp.einsum("scka,aj->sckj", spec_imag, col_real, precision=HIGH) - jnp.einsum(
        "scka,aj->sckj", spec_real, col_imag, precision=HIGH
    )
    turned_real = section_real * twist_real + section_imag * twist_imag
    turned_imag = section_imag * twist_real - section_real * twist_imag
    signal = jnp.einsum(
        "nk,scka->snac", row_real[:half_rows], turned_real, precision=HIGH
    ) + jnp.einsum("nk,scka->snac", row_imag[:half_rows], turned_imag, precision=HIGH)
    return signal.reshape(signal.shape[0], half_rows * columns, signal.shape[3]) * (1.0 / padded)


def times_spec(first, second):
    return (
        first[0] * second[0] - first[1] * second[1],
        first[0] * second[1] + first[1] * second[0],
    )


def times_conj(first, second):
    return (
        first[0] * second[0] + first[1] * second[1],
        first[1] * second[0] - first[0] * second[1],
    )


def local(query, key_input, value_input, filter_taps, grad_output):
    product = (key_input.astype(jnp.float32) * value_input.astype(jnp.float32)).astype(jnp.bfloat16)
    grad_mix = (grad_output.astype(jnp.float32) * query.astype(jnp.float32)).astype(jnp.bfloat16)
    owned_filter = lax.all_to_all(filter_taps, "ctx", split_axis=1, concat_axis=0, tiled=True)
    tables = build_tables(owned_filter.shape[0])
    filter_spec = forward(owned_filter[None], tables)
    local_product = lax.all_to_all(product, "ctx", split_axis=2, concat_axis=1, tiled=True)
    prod_spec = forward(local_product.astype(jnp.float32), tables)
    owned_mixed = inverse(times_spec(filter_spec, prod_spec), tables).astype(jnp.bfloat16)
    owned_mixed, prod_spec = (owned_mixed, prod_spec)
    mixed = lax.all_to_all(owned_mixed, "ctx", split_axis=1, concat_axis=2, tiled=True)
    owned_grad = lax.all_to_all(grad_mix, "ctx", split_axis=2, concat_axis=1, tiled=True)
    grad_spec = forward(owned_grad.astype(jnp.float32), tables)
    owned_back = inverse(times_conj(grad_spec, filter_spec), tables).astype(jnp.bfloat16)
    taps_spec = times_conj(grad_spec, prod_spec)
    owned_back, taps_spec = (
        owned_back,
        (jnp.sum(taps_spec[0], axis=0), jnp.sum(taps_spec[1], axis=0)),
    )
    grad_product = lax.all_to_all(owned_back, "ctx", split_axis=1, concat_axis=2, tiled=True)
    mixed_wide = mixed.astype(jnp.float32)
    back_wide = grad_product.astype(jnp.float32)
    output = (query.astype(jnp.float32) * mixed_wide).astype(jnp.bfloat16)
    grad_query = (grad_output.astype(jnp.float32) * mixed_wide).astype(jnp.bfloat16)
    grad_key = (back_wide * value_input.astype(jnp.float32)).astype(jnp.bfloat16)
    grad_value = (back_wide * key_input.astype(jnp.float32)).astype(jnp.bfloat16)
    local_taps = inverse((taps_spec[0][None], taps_spec[1][None]), tables)[0]
    owned_taps = lax.psum(local_taps, "dp")
    grad_filter = lax.all_to_all(owned_taps, "ctx", split_axis=0, concat_axis=1, tiled=True)
    return (output, grad_query, grad_key, grad_value, grad_filter)


def plan(mesh, query, key_input, value_input, filter_taps, grad_output):
    nctx, ndp = mesh.shape["ctx"], mesh.shape["dp"]
    sequences, length, channels = query.shape
    fits = 2 * channels == nctx * LANES and nctx == 2 * ndp and sequences == 1 and length % 32 == 0 and length <= LANES
    run = functools.partial(fused, nctx, ndp) if fits else local
    return run(query, key_input, value_input, filter_taps, grad_output)


def solution(mesh):
    wide, taps = P("dp", "ctx", None), P("ctx", None)
    return jax.shard_map(
        functools.partial(plan, mesh),
        mesh=mesh,
        in_specs=(wide, wide, wide, taps, wide),
        out_specs=(wide, wide, wide, wide, taps),
        check_vma=False,
    )
```

profile of v0, /device:TPU:0, one launch (start us, length us, event | category | flops | bytes accessed | tf_op | source)
XLA Modules:
  0.0 31.6 jit_solution(13330898816918311548)
XLA Ops:
  0.6 26.4 %shard_map.110 = (bf16[1,128,512]{2,1,0:T(8,128)(2,1)}, bf16[1,128,512]{2,1,0:T(8,128)(2,1)}, bf16[1,128,512]{2,1,0:T(8,128)(2,1)}, bf16[1,128,512]{2,1,0:T(8,128)(2,1)}, f32[128,512]{1,0:T(8,128)}) custom-call(bf16[1,128,512]{2,1,0:T(8,128)(2,1)} %q_ref.1, bf16[1,128,512]{2,1,0:T(8,128)(2,1)} %k_ref.1, bf16[1,128,512]{2,1,0:T(8,128)(2,1)} %v_ref.1, ...), custom_call_target="tpu_custom_call" | custom-call | tf_op jit(solution)/shard_map/pallas_call | solution.py:313
  27.1 0.0 copy-start.3
  27.1 1.6 %copy.17 = bf16[1,128,512]{2,1,0:T(8,128)(2,1)} copy(bf16[1,128,512]{2,1,0:T(8,128)(2,1)} %get-tuple-element.10) | data formatting | bytes 262144
  28.7 0.0 copy-done.3
  28.7 0.0 copy-start.2
  28.7 0.0 copy-start.1
  28.7 0.7 %copy.18 = bf16[1,128,512]{2,1,0:T(8,128)(2,1)} copy(bf16[1,128,512]{2,1,0:T(8,128)(2,1)S(1)} %copy-done.3) | data formatting | bytes 262144
  29.3 0.3 copy-done.2
  29.6 0.0 copy-start
  29.6 0.7 %copy.19 = bf16[1,128,512]{2,1,0:T(8,128)(2,1)} copy(bf16[1,128,512]{2,1,0:T(8,128)(2,1)S(1)} %copy-done.2) | data formatting | bytes 262144
  30.3 0.0 copy-done.1
  30.3 0.7 %copy.20 = bf16[1,128,512]{2,1,0:T(8,128)(2,1)} copy(bf16[1,128,512]{2,1,0:T(8,128)(2,1)S(1)} %copy-done.1) | data formatting | bytes 262144
  30.9 0.0 copy-done
  30.9 0.7 %copy.21 = f32[128,512]{1,0:T(8,128)} copy(f32[128,512]{1,0:T(8,128)S(1)} %copy-done) | data formatting | bytes 524288
Async XLA Ops:
  27.1 1.6 %copy-start.3 = (bf16[1,128,512]{2,1,0:T(8,128)(2,1)S(1)}, bf16[1,128,512]{2,1,0:T(8,128)(2,1)}, u32[]{:S(2)}) copy-start(bf16[1,128,512]{2,1,0:T(8,128)(2,1)} %get-tuple-element.11) | copy-start | bytes 393220
  28.7 1.0 %copy-start.2 = (bf16[1,128,512]{2,1,0:T(8,128)(2,1)S(1)}, bf16[1,128,512]{2,1,0:T(8,128)(2,1)}, u32[]{:S(2)}) copy-start(bf16[1,128,512]{2,1,0:T(8,128)(2,1)} %get-tuple-element.12) | copy-start | bytes 393220
  28.7 1.6 %copy-start.1 = (bf16[1,128,512]{2,1,0:T(8,128)(2,1)S(1)}, bf16[1,128,512]{2,1,0:T(8,128)(2,1)}, u32[]{:S(2)}) copy-start(bf16[1,128,512]{2,1,0:T(8,128)(2,1)} %get-tuple-element.13) | copy-start | bytes 393220
  29.6 1.3 %copy-start = (f32[128,512]{1,0:T(8,128)S(1)}, f32[128,512]{1,0:T(8,128)}, u32[]{:S(2)}) copy-start(f32[128,512]{1,0:T(8,128)} %get-tuple-element.14) | copy-start | bytes 786436
where the time goes:
time: 31.8 us; the launch traced here: 31.6 us
  Pallas kernels  26.4 us (83%)
  local copies, waits for them, and re-layouts  4.58 us (14%)
  between operations  0.65 us (2%)
    pallas_call x1, Pallas kernels, fused(): pl.pallas_call(functools.partial(kernel, nctx, ndp), out_shape=(wide, wid...  26.4 us
    unnamed x13, local copies, waits for them, and re-layouts  4.58 us

commit v1 on v0

--- a/solution.py
+++ b/solution.py
@@ -12,6 +12,7 @@
 HIGH = lax.Precision.HIGHEST
 MESH = pl.DeviceIdType.MESH
 LANES = 128
+VMEM_BYTES = 67043328
 F32 = jnp.float32
 BF16 = jnp.bfloat16
 
@@ -45,20 +46,26 @@
 def kernel(
     nctx,
     ndp,
-    q_ref,
-    k_ref,
-    v_ref,
-    f_ref,
-    g_ref,
-    ahead_ref,
-    back_ref,
-    out_ref,
-    gq_ref,
-    gk_ref,
-    gv_ref,
-    gf_ref,
+    q_hbm,
+    k_hbm,
+    v_hbm,
+    f_hbm,
+    g_hbm,
+    ahead_hbm,
+    back_hbm,
+    mg_rx,
+    g2_rx,
+    qv,
+    kv,
+    vv,
+    gv,
+    fv,
+    ahead_v,
+    back_v,
     send1,
     rx1,
+    sendf,
+    rxf,
     sig,
     wei,
     oth,
@@ -66,11 +73,12 @@
     rs_send,
     rs_rx,
     g2_send,
-    g2_rx,
     mg_send,
-    mg_rx,
+    load_sem,
     s1_send,
     s1_recv,
+    sf_send,
+    sf_recv,
     rs_ssem,
     rs_rsem,
     g2_ssem,
@@ -80,14 +88,19 @@
 ):
     me = lax.axis_index("ctx")
     row = lax.axis_index("dp")
-    length = q_ref.shape[1]
+    length = qv.shape[1]
     hl = length // 2
     tiles = nctx // 2
+
+    pairs = ((k_hbm, kv), (v_hbm, vv), (g_hbm, gv), (q_hbm, qv), (f_hbm, fv), (ahead_hbm, ahead_v), (back_hbm, back_v))
+    loads = [pltpu.make_async_copy(src, dst, load_sem.at[n]) for n, (src, dst) in enumerate(pairs)]
+    for load in loads:
+        load.start()
 
     barrier = pltpu.get_barrier_semaphore()
     for oc in range(nctx):
         for od in range(ndp):
-            if oc or od:
+            if (oc == 0) != (od == 0):
                 pl.semaphore_signal(
                     barrier,
                     inc=1,
@@ -97,18 +110,17 @@
 
     low = lax.broadcasted_iota(jnp.int32, (length, LANES), 1) < LANES // 2
     low_h = lax.broadcasted_iota(jnp.int32, (hl, LANES), 1) < LANES // 2
+    for load in loads[:4]:
+        load.wait()
     for p in range(tiles):
         cols = slice(p * LANES, (p + 1) * LANES)
-        x = (k_ref[0, :, cols].astype(F32) * v_ref[0, :, cols].astype(F32)).astype(BF16).astype(F32)
-        g = (g_ref[0, :, cols].astype(F32) * q_ref[0, :, cols].astype(F32)).astype(BF16).astype(F32)
+        x = (kv[0, :, cols].astype(F32) * vv[0, :, cols].astype(F32)).astype(BF16).astype(F32)
+        g = (gv[0, :, cols].astype(F32) * qv[0, :, cols].astype(F32)).astype(BF16).astype(F32)
         even, odd = merge(x, g, low)
-        send1[2 * p, 0:length, :] = even.astype(BF16)
-        send1[2 * p + 1, 0:length, :] = odd.astype(BF16)
-        even, odd = merge(f_ref[0:hl, cols], f_ref[hl:length, cols], low_h)
-        send1[2 * p, length : length + hl, :] = even.astype(BF16)
-        send1[2 * p + 1, length : length + hl, :] = odd.astype(BF16)
-
-    pl.semaphore_wait(barrier, nctx * ndp - 1)
+        send1[2 * p] = even.astype(BF16)
+        send1[2 * p + 1] = odd.astype(BF16)
+
+    pl.semaphore_wait(barrier, nctx + ndp - 2)
 
     def copy1(peer, slot):
         return pltpu.make_async_remote_copy(
@@ -120,26 +132,44 @@
             device_id_type=MESH,
         )
 
+    def copyf(peer, slot):
+        return pltpu.make_async_remote_copy(
+            src_ref=sendf.at[peer],
+            dst_ref=rxf.at[slot],
+            send_sem=sf_send.at[peer],
+            recv_sem=sf_recv.at[slot],
+            device_id={"ctx": peer, "dp": row},
+            device_id_type=MESH,
+        )
+
     order = [nctx // 2 + o for o in range(nctx // 2)] + list(range(1, nctx // 2))
     peers = [lax.rem(me + o, nctx) for o in order]
     for peer in peers:
         copy1(peer, me).start()
-    rx1[pl.ds(me, 1)] = send1[pl.ds(me, 1)]
-
-    def transform(src):
-        z = rx1[src, 0:length, :]
-        fa = rx1[src, length : length + hl, :].astype(F32)
+    loads[4].wait()
+    for p in range(tiles):
+        cols = slice(p * LANES, (p + 1) * LANES)
+        even, odd = merge(fv[0:hl, cols], fv[hl:length, cols], low_h)
+        sendf[2 * p] = even.astype(BF16)
+        sendf[2 * p + 1] = odd.astype(BF16)
+    for load in loads[5:]:
+        load.wait()
+    for peer in peers:
+        copyf(peer, me).start()
+
+    def transform(z):
+        return jnp.dot(ahead_v[...], jnp.concatenate([z, z], axis=0), preferred_element_type=F32)
+
+    def weigh(fa):
+        fa = fa.astype(F32)
         turned = pltpu.roll(fa, LANES // 2, 1)
-        w = jnp.concatenate([jnp.where(low_h, fa, turned), jnp.where(low_h, turned, fa)], axis=0).astype(BF16)
-        both = jnp.concatenate([z, w], axis=1)
-        spec = jnp.dot(ahead_ref[...], jnp.concatenate([both, both], axis=0), preferred_element_type=F32)
-        sig[src] = spec[:, 0:LANES]
-        wei[src] = spec[:, LANES:]
-
-    transform(me)
+        w = jnp.concatenate([jnp.where(low_h, fa, turned), jnp.where(low_h, turned, fa)], axis=0)
+        return transform(w.astype(BF16))
+
+    sig[me] = transform(send1[me])
     for peer in reversed(peers):
         copy1(peer, peer).wait_recv()
-        transform(peer)
+        sig[peer] = transform(rx1[peer])
 
     lane8 = lax.broadcasted_iota(jnp.int32, (8, LANES), 1) < LANES // 2
     parity = lax.rem(lax.broadcasted_iota(jnp.int32, (8, LANES), 0), 2)
@@ -174,7 +204,7 @@
 
     def inverse(spec):
         high = spec.astype(BF16)
-        return jnp.dot(back_ref[...], jnp.concatenate([high, high], axis=0), preferred_element_type=F32)
+        return jnp.dot(back_v[...], jnp.concatenate([high, high], axis=0), preferred_element_type=F32)
 
     def copy_rs(peer, slot):
         return pltpu.make_async_remote_copy(
@@ -191,6 +221,11 @@
     rows_peers = [lax.rem(row + o, ndp) for o in range(1, ndp)]
     for peer in rows_peers:
         copy_rs(peer, row).start()
+
+    wei[me] = weigh(sendf[me])
+    for peer in reversed(peers):
+        copyf(peer, peer).wait_recv()
+        wei[peer] = weigh(rxf[peer])
 
     @pl.loop(0, length // 8)
     def _(i):
@@ -267,13 +302,6 @@
 
     for peer in peers:
         copy_mg(peer, peer).wait_recv()
-    for p in range(tiles):
-        cols = slice(p * LANES, (p + 1) * LANES)
-        mixed, back = merge(mg_rx[2 * p].astype(F32), mg_rx[2 * p + 1].astype(F32), low)
-        out_ref[0, :, cols] = (q_ref[0, :, cols].astype(F32) * mixed).astype(BF16)
-        gq_ref[0, :, cols] = (g_ref[0, :, cols].astype(F32) * mixed).astype(BF16)
-        gk_ref[0, :, cols] = (v_ref[0, :, cols].astype(F32) * back).astype(BF16)
-        gv_ref[0, :, cols] = (k_ref[0, :, cols].astype(F32) * back).astype(BF16)
 
     from_row = lax.rem(me, tiles)
     for c in range(nctx):
@@ -283,14 +311,9 @@
         def _():
             copy_g2(0, row, c).wait_recv()
 
-    for p in range(tiles):
-        cols = slice(p * LANES, (p + 1) * LANES)
-        top, bottom = merge(g2_rx[2 * p].astype(F32), g2_rx[2 * p + 1].astype(F32), low_h)
-        gf_ref[0:hl, cols] = top
-        gf_ref[hl:length, cols] = bottom
-
     for peer in peers:
         copy1(peer, me).wait_send()
+        copyf(peer, me).wait_send()
         copy_mg(peer, me).wait_send()
     for peer in rows_peers:
         copy_rs(peer, row).wait_send()
@@ -303,21 +326,64 @@
             copy_g2(part, row, me).wait_send()
 
 
+def finish(mg, g2, q, k, v, g, out_hbm, gq_hbm, gk_hbm, gv_hbm, gf_hbm, out_v, gq_v, gk_v, gv_v, gf_v, sems):
+    length = q.shape[1]
+    hl = length // 2
+    tiles = mg.shape[0] // 2
+    low = lax.broadcasted_iota(jnp.int32, (length, LANES), 1) < LANES // 2
+    low_h = lax.broadcasted_iota(jnp.int32, (hl, LANES), 1) < LANES // 2
+    copies = []
+
+    def put(n, p, src, dst):
+        copy = pltpu.make_async_copy(src, dst, sems.at[n, p])
+        copy.start()
+        copies.append(copy)
+
+    for p in range(tiles):
+        cols = slice(p * LANES, (p + 1) * LANES)
+        mixed, back = merge(mg[2 * p].astype(F32), mg[2 * p + 1].astype(F32), low)
+        out_v[0, :, cols] = (q[0, :, cols].astype(F32) * mixed).astype(BF16)
+        gq_v[0, :, cols] = (g[0, :, cols].astype(F32) * mixed).astype(BF16)
+        gk_v[0, :, cols] = (v[0, :, cols].astype(F32) * back).astype(BF16)
+        gv_v[0, :, cols] = (k[0, :, cols].astype(F32) * back).astype(BF16)
+        top, bottom = merge(g2[2 * p].astype(F32), g2[2 * p + 1].astype(F32), low_h)
+        gf_v[0:hl, cols] = top
+        gf_v[hl:length, cols] = bottom
+        for n, (src, dst) in enumerate(((out_v, out_hbm), (gq_v, gq_hbm), (gk_v, gk_hbm), (gv_v, gv_hbm))):
+            put(n, p, src.at[:, :, cols], dst.at[:, :, cols])
+        put(4, p, gf_v.at[:, cols], gf_hbm.at[:, cols])
+    for copy in copies:
+        copy.wait()
+
+
 def fused(nctx, ndp, query, key_input, value_input, filter_taps, grad_output):
     length, channels = query.shape[1], query.shape[2]
     ahead, back = block_tables(length)
     vm = pl.BlockSpec(memory_space=pltpu.VMEM)
-    wide = jax.ShapeDtypeStruct(query.shape, BF16)
+    hbm = pl.BlockSpec(memory_space=pltpu.HBM)
     hl, tiles = length // 2, nctx // 2
     dma = pltpu.SemaphoreType.DMA
-    return pl.pallas_call(
+    kept = 2 * (4 * query.size + nctx * (length + hl) * LANES) + 16384
+    arrived = pl.pallas_call(
         functools.partial(kernel, nctx, ndp),
-        out_shape=(wide, wide, wide, wide, jax.ShapeDtypeStruct((length, channels), F32)),
-        in_specs=[vm] * 7,
-        out_specs=(vm,) * 5,
+        out_shape=(
+            pltpu.VMEM((nctx, length, LANES), BF16),
+            pltpu.VMEM((nctx, hl, LANES), BF16),
+            pltpu.VMEM(query.shape, BF16),
+            pltpu.VMEM(query.shape, BF16),
+            pltpu.VMEM(query.shape, BF16),
+            pltpu.VMEM(query.shape, BF16),
+        ),
+        in_specs=[hbm] * 7,
+        out_specs=(vm,) * 6,
         scratch_shapes=[
-            pltpu.VMEM((nctx, length + hl, LANES), BF16),
-            pltpu.VMEM((nctx, length + hl, LANES), BF16),
+            pltpu.VMEM((length, channels), F32),
+            pltpu.VMEM(ahead.shape, BF16),
+            pltpu.VMEM(back.shape, BF16),
+            pltpu.VMEM((nctx, length, LANES), BF16),
+            pltpu.VMEM((nctx, length, LANES), BF16),
+            pltpu.VMEM((nctx, hl, LANES), BF16),
+            pltpu.VMEM((nctx, hl, LANES), BF16),
             pltpu.VMEM((nctx, 2 * length, LANES), F32),
             pltpu.VMEM((nctx, 2 * length, LANES), F32),
             pltpu.VMEM((nctx, 2 * length, LANES), F32),
@@ -325,9 +391,10 @@
             pltpu.VMEM((tiles, length, LANES), BF16),
             pltpu.VMEM((ndp, length, LANES), BF16),
             pltpu.VMEM((2, hl, LANES), BF16),
-            pltpu.VMEM((nctx, hl, LANES), BF16),
             pltpu.VMEM((nctx, length, LANES), BF16),
-            pltpu.VMEM((nctx, length, LANES), BF16),
+            dma((7,)),
+            dma((nctx,)),
+            dma((nctx,)),
             dma((nctx,)),
             dma((nctx,)),
             dma((ndp,)),
@@ -337,8 +404,19 @@
             dma((nctx,)),
             dma((nctx,)),
         ],
-        compiler_params=pltpu.CompilerParams(collective_id=0, has_side_effects=True),
+        compiler_params=pltpu.CompilerParams(
+            collective_id=0, has_side_effects=True, vmem_limit_bytes=VMEM_BYTES - kept
+        ),
     )(query, key_input, value_input, filter_taps, grad_output, jnp.asarray(ahead), jnp.asarray(back))
+    wide = jax.ShapeDtypeStruct(query.shape, BF16)
+    return pl.pallas_call(
+        finish,
+        out_shape=(wide, wide, wide, wide, jax.ShapeDtypeStruct((length, channels), F32)),
+        in_specs=[vm] * 6,
+        out_specs=(hbm,) * 5,
+        scratch_shapes=[pltpu.VMEM(query.shape, BF16)] * 4 + [pltpu.VMEM((length, channels), F32), dma((5, tiles))],
+        compiler_params=pltpu.CompilerParams(vmem_limit_bytes=16 * 1024 * 1024),
+    )(*arrived)
 
 
 def build_tables(length):

time: 31.8 us -> 26.1 us (0.82)
  local copies, waits for them, and re-layouts: 4.58 us -> 0 us
  Pallas kernels: 26.4 us -> 25.3 us
    unnamed x13 -> x0, local copies, waits for them, and re-layouts: 4.58 us -> none
    pallas_call x1 -> x2, Pallas kernels: 26.4 us -> 25.3 us  [the longest x1 24.2 us: fused(): pl.pallas_call(functools.partial(kernel, nctx, ndp), out_shape=(pltpu.VME...]
where the time goes in v1:
time: 26.1 us; the launch traced here: 26 us
  Pallas kernels  25.3 us (97%)
  between operations  0.64 us (2%)
    pallas_call x1, Pallas kernels, fused(): pl.pallas_call(functools.partial(kernel, nctx, ndp), out_shape=(pltpu.VME...  24.2 us
    pallas_call x1, Pallas kernels, fused(): pl.pallas_call(finish, out_shape=(wide, wide, wide, wide, jax.ShapeDtypeS...  1.15 us

profile of v1, /device:TPU:0, one launch (start us, length us, event | category | flops | bytes accessed | tf_op | source)
XLA Modules:
  0.0 26.0 jit_solution(18040308512750655553)
XLA Ops:
  0.6 24.2 %shard_map.110 = (bf16[8,128,128]{2,1,0:T(8,128)(2,1)S(1)}, bf16[8,64,128]{2,1,0:T(8,128)(2,1)S(1)}, bf16[1,128,512]{2,1,0:T(8,128)(2,1)S(1)}, bf16[1,128,512]{2...) custom-call(bf16[1,128,512]{2,1,0:T(8,128)(2,1)} %q_hbm.1, ...), custom_call_target="tpu_custom_call" | custom-call | tf_op jit(solution)/shard_map/pallas_call | solution.py:367
  24.8 1.2 %shard_map.111 = (bf16[1,128,512]{2,1,0:T(8,128)(2,1)}, bf16[1,128,512]{2,1,0:T(8,128)(2,1)}, bf16[1,128,512]{2,1,0:T(8,128)(2,1)}, bf16[1,128,512]{2,1,0:T(8,128)(2,1)}, f32[128,512]{1,0:T(8,128)}) custom-call(bf16[8,128,128]{2,1,0:T(8,128)(2,1)S(1)} %get-tuple-element.11.mg, bf16[8,64,128]{2,1,0:T(8,128)(2,1)S(1)} %get-tuple-element.12.g2, ...), custom_call_target="tpu_custom_call" | custom-call | tf_op jit(solution)/shard_map/pallas_call | solution.py:412

commit v2 on v1

--- a/solution.py
+++ b/solution.py
@@ -74,6 +74,7 @@
     rs_rx,
     g2_send,
     mg_send,
+    known,
     load_sem,
     s1_send,
     s1_recv,
@@ -98,15 +99,15 @@
         load.start()
 
     barrier = pltpu.get_barrier_semaphore()
-    for oc in range(nctx):
-        for od in range(ndp):
-            if (oc == 0) != (od == 0):
-                pl.semaphore_signal(
-                    barrier,
-                    inc=1,
-                    device_id={"ctx": lax.rem(me + oc, nctx), "dp": lax.rem(row + od, ndp)},
-                    device_id_type=MESH,
-                )
+    for oc in range(1, nctx):
+        pl.semaphore_signal(
+            barrier, inc=1, device_id={"ctx": lax.rem(me + oc, nctx), "dp": row}, device_id_type=MESH
+        )
+    for step, there in ((1, row + 1 < ndp), (-1, row > 0)):
+
+        @pl.when(there)
+        def _(step=step):
+            pl.semaphore_signal(barrier, inc=1, device_id={"ctx": me, "dp": row + step}, device_id_type=MESH)
 
     low = lax.broadcasted_iota(jnp.int32, (length, LANES), 1) < LANES // 2
     low_h = lax.broadcasted_iota(jnp.int32, (hl, LANES), 1) < LANES // 2
@@ -120,7 +121,8 @@
         send1[2 * p] = even.astype(BF16)
         send1[2 * p + 1] = odd.astype(BF16)
 
-    pl.semaphore_wait(barrier, nctx + ndp - 2)
+    beside = jnp.where(row + 1 < ndp, 1, 0) + jnp.where(row > 0, 1, 0)
+    pl.semaphore_wait(barrier, nctx - 1 + beside)
 
     def copy1(peer, slot):
         return pltpu.make_async_remote_copy(
@@ -146,6 +148,18 @@
     peers = [lax.rem(me + o, nctx) for o in order]
     for peer in peers:
         copy1(peer, me).start()
+    for n, (step, dist) in enumerate(((1, row), (-1, ndp - 1 - row))):
+
+        @pl.when(dist >= 2)
+        def _(n=n):
+            pl.semaphore_wait(known.at[n], 1)
+
+        @pl.when(jnp.logical_and(dist >= 1, dist + 1 < ndp))
+        def _(n=n, step=step):
+            pl.semaphore_signal(
+                known.at[n], inc=1, device_id={"ctx": me, "dp": row + step}, device_id_type=MESH
+            )
+
     loads[4].wait()
     for p in range(tiles):
         cols = slice(p * LANES, (p + 1) * LANES)
@@ -392,6 +406,7 @@
             pltpu.VMEM((ndp, length, LANES), BF16),
             pltpu.VMEM((2, hl, LANES), BF16),
             pltpu.VMEM((nctx, length, LANES), BF16),
+            pltpu.SemaphoreType.REGULAR((2,)),
             dma((7,)),
             dma((nctx,)),
             dma((nctx,)),

time: 26.1 us -> 24.1 us (0.923)
  Pallas kernels: 25.3 us -> 23.3 us
    pallas_call x1, Pallas kernels: 24.2 us -> 22.2 us  [fused(): pl.pallas_call(functools.partial(kernel, nctx, ndp), out_shape=(pltpu.VME...]
where the time goes in v2:
time: 24.1 us; the launch traced here: 23.9 us
  Pallas kernels  23.3 us (97%)
  between operations  0.64 us (3%)
    pallas_call x1, Pallas kernels, fused(): pl.pallas_call(functools.partial(kernel, nctx, ndp), out_shape=(pltpu.VME...  22.2 us
    pallas_call x1, Pallas kernels, fused(): pl.pallas_call(finish, out_shape=(wide, wide, wide, wide, jax.ShapeDtypeS...  1.15 us

profile of v2, /device:TPU:0, one launch (start us, length us, event | category | flops | bytes accessed | tf_op | source)
XLA Modules:
  0.0 23.9 jit_solution(297461913432135934)
XLA Ops:
  0.6 22.2 %shard_map.110 = (bf16[8,128,128]{2,1,0:T(8,128)(2,1)S(1)}, bf16[8,64,128]{2,1,0:T(8,128)(2,1)S(1)}, bf16[1,128,512]{2,1,0:T(8,128)(2,1)S(1)}, bf16[1,128,512]{2...) custom-call(bf16[1,128,512]{2,1,0:T(8,128)(2,1)} %q_hbm.1, ...), custom_call_target="tpu_custom_call" | custom-call | tf_op jit(solution)/shard_map/pallas_call | solution.py:381
  22.8 1.2 %shard_map.111 = (bf16[1,128,512]{2,1,0:T(8,128)(2,1)}, bf16[1,128,512]{2,1,0:T(8,128)(2,1)}, bf16[1,128,512]{2,1,0:T(8,128)(2,1)}, bf16[1,128,512]{2,1,0:T(8,128)(2,1)}, f32[128,512]{1,0:T(8,128)}) custom-call(bf16[8,128,128]{2,1,0:T(8,128)(2,1)S(1)} %get-tuple-element.11.mg, bf16[8,64,128]{2,1,0:T(8,128)(2,1)S(1)} %get-tuple-element.12.g2, ...), custom_call_target="tpu_custom_call" | custom-call | tf_op jit(solution)/shard_map/pallas_call | solution.py:427
